TPU v7x, 32 devices: a whole 2x2x4 slice. The times are simulated.
32 devices in a mesh: ka: 8 (over z, y), ga: 4 (over x, core).
Axes of the slice: x: 2, y: 2, z: 4, core: 2. Of those that a mesh axis runs over, the one named last changes fastest.
Arguments:
- x_dens: bfloat16 [32, 64, 1500], P('ka', None, 'ga'), may hold values from -6 to 6
- y_dens: bfloat16 [32, 64, 1500], P('ka', None, 'ga'), may hold values from -0.15625 to 0.15625
- p_dens: bfloat16 [32, 64, 1500], P('ka', None, 'ga'), may hold values from -1 to 1
- coulomb: float32 [1500], P('ga'), may hold values from 0.1 to 2
- screened: bfloat16 [16, 1500, 1500], P('ka', 'ga'), may hold values from -0.15625 to 0.15625
- pairs: int32 [128, 3], P('ka'), may hold values from 0 to 31, as said below
- q_slot: int32 [16], replicated, may hold values from 0 to 15, as said below
Outputs:
- blocks: float32 [128, 4096], P('ka')
- mirrored: float32 [32, 4096], P('ka')
Inputs may be any that keep to these rules, and one draw needn't show every extreme that they name: `pairs`: column 0 of the rows held by index d of ka lies in d * 4 to (d + 1) * 4 - 1; column 1 is any k-point; column 2 is a momentum transfer below 16. Among one index's 16 rows at most 2 have a second k-point held by one same index, and this is reached; at most 2 have q_slot[q] // 2 equal to one same value, and this is reached. `q_slot`: A permutation of the slots; slot s of screened is held by index s // 2 of ka.
All inputs are finite; a program needn't handle non-finite values.
Results may differ from a plain program's by a relative error of at most 0.0014.
Values may be sent and summed in bfloat16 or wider, within the bound.
A program may use at most 192 MiB of HBM per device.

v0:
```python
import jax
import jax.numpy as jnp
from jax import lax
from jax.sharding import PartitionSpec as P

CAPQ = 2
CAPK = 2


def earlier_count(owners):
    places = jnp.arange(owners.shape[0])
    same_owner = owners[:, None] == owners[None, :]
    before = places[:, None] > places[None, :]
    return jnp.sum(jnp.logical_and(same_owner, before).astype(jnp.int32), axis=1)


def per_device(x_dens, y_dens, p_dens, coulomb, screened, pairs, q_slot):
    n_ka = lax.axis_size("ka")
    mine_index = lax.axis_index("ka")
    per_dev, transitions, g_local = x_dens.shape
    q_slots = screened.shape[0]
    pair_rows = pairs.shape[0]
    k_local = pairs[:, 0] - mine_index * per_dev
    partner = pairs[:, 1]
    q_index = pairs[:, 2]
    slot_of = jnp.sum(
        jnp.where(q_index[:, None] == jnp.arange(q_slot.shape[0])[None, :], q_slot[None, :], 0),
        axis=1,
    )
    q_owner = slot_of // q_slots
    q_local = slot_of % q_slots
    q_rank = earlier_count(q_owner)
    q_route = ((q_owner * CAPQ + q_rank)[:, None] == jnp.arange(n_ka * CAPQ)[None, :]).astype(
        jnp.bfloat16
    )
    pick_first = (k_local[:, None] == jnp.arange(per_dev)[None, :]).astype(jnp.bfloat16)
    x_rows = jnp.einsum(
        "jk,kig->jig", pick_first, x_dens, preferred_element_type=jnp.float32
    ).astype(jnp.bfloat16)
    p_rows = jnp.einsum(
        "jk,kig->jig", pick_first, p_dens, preferred_element_type=jnp.float32
    ).astype(jnp.bfloat16)
    send_x = jnp.einsum("js,jig->sig", q_route, x_rows, preferred_element_type=jnp.float32).astype(
        jnp.bfloat16
    )
    send_x = send_x.reshape(n_ka, CAPQ, transitions, g_local)
    send_q = jnp.sum(q_route.astype(jnp.int32) * q_local[:, None], axis=0).reshape(n_ka, CAPQ)
    got_x, got_q = (
        lax.all_to_all(send_x, "ka", split_axis=0, concat_axis=0, tiled=True),
        lax.all_to_all(send_q, "ka", split_axis=0, concat_axis=0, tiled=True),
    )
    chosen = (got_q[:, :, None] == jnp.arange(q_slots)[None, None, :]).astype(jnp.bfloat16)
    stacked = got_x[:, :, None, :, :] * chosen[:, :, :, None, None]
    partial_value = jnp.einsum(
        "ncsig,sgh->hnci", stacked, screened, preferred_element_type=jnp.float32
    )
    half_rows = lax.psum_scatter(
        partial_value.reshape(lax.axis_size("ga") * g_local, n_ka, CAPQ * transitions),
        "ga",
        scatter_dimension=0,
        tiled=True,
    ).astype(jnp.bfloat16)
    returned = lax.all_to_all(half_rows, "ka", split_axis=1, concat_axis=1, tiled=True)
    returned = returned.reshape(g_local, n_ka * CAPQ, transitions)
    u_rows = jnp.einsum(
        "js,gsi->jig", q_route, returned, preferred_element_type=jnp.float32
    ).astype(jnp.bfloat16)
    all_pairs = lax.all_gather(pairs, "ka", axis=0, tiled=True).reshape(n_ka, pair_rows, 3)
    seconds = all_pairs[:, :, 1]
    k_owners = seconds // per_dev
    k_ranks = jax.vmap(earlier_count)(k_owners)
    held_here = k_owners == mine_index
    rank_hot = (k_ranks[:, :, None] == jnp.arange(CAPK)[None, None, :]).astype(jnp.float32)
    local_hot = jnp.logical_and(
        (seconds - mine_index * per_dev)[:, :, None] == jnp.arange(per_dev)[None, None, :],
        held_here[:, :, None],
    ).astype(jnp.float32)
    selector = jnp.einsum("njc,njk->nck", rank_hot, local_hot).astype(jnp.bfloat16)
    send_y = jnp.einsum(
        "nck,kig->ncig", selector, y_dens, preferred_element_type=jnp.float32
    ).astype(jnp.bfloat16)
    send_p = jnp.einsum(
        "nck,kig->ncig", selector, p_dens, preferred_element_type=jnp.float32
    ).astype(jnp.bfloat16)
    got_y, got_p = (
        lax.all_to_all(send_y, "ka", split_axis=0, concat_axis=0, tiled=True),
        lax.all_to_all(send_p, "ka", split_axis=0, concat_axis=0, tiled=True),
    )
    own_rank = earlier_count(partner // per_dev)
    pick_second = (
        (partner // per_dev * CAPK + own_rank)[:, None] == jnp.arange(n_ka * CAPK)[None, :]
    ).astype(jnp.bfloat16)
    y_rows = jnp.einsum(
        "js,sig->jig",
        pick_second,
        got_y.reshape(n_ka * CAPK, transitions, g_local),
        preferred_element_type=jnp.float32,
    ).astype(jnp.bfloat16)
    pp_rows = jnp.einsum(
        "js,sig->jig",
        pick_second,
        got_p.reshape(n_ka * CAPK, transitions, g_local),
        preferred_element_type=jnp.float32,
    ).astype(jnp.bfloat16)
    direct = jnp.einsum("jig,jhg->jih", u_rows, y_rows, preferred_element_type=jnp.float32)
    weighted = p_rows.astype(jnp.float32) * coulomb[None, None, :]
    exchange_term = jnp.einsum(
        "jig,jhg->jih", weighted, pp_rows.astype(jnp.float32), precision=lax.Precision.HIGHEST
    )
    kernel_block = lax.psum(2.0 * exchange_term - direct, "ga")
    blocks = kernel_block.reshape(pair_rows, transitions * transitions)
    flipped = jnp.transpose(kernel_block, (0, 2, 1)).reshape(pair_rows, transitions * transitions)
    selector = (partner[:, None] == jnp.arange(lax.axis_size("ka") * per_dev)[None, :]).astype(
        jnp.float32
    )
    mirrored = lax.psum_scatter(
        jnp.dot(selector.T, flipped, precision=lax.Precision.HIGHEST),
        "ka",
        scatter_dimension=0,
        tiled=True,
    )
    return (blocks, mirrored)


def solution(mesh):
    in_specs = (
        P("ka", None, "ga"),
        P("ka", None, "ga"),
        P("ka", None, "ga"),
        P("ga"),
        P("ka", "ga", None),
        P("ka", None),
        P(),
    )
    out_specs = (P("ka", None), P("ka", None))
    return jax.shard_map(
        per_device, mesh=mesh, in_specs=in_specs, out_specs=out_specs, check_vma=False
    )
```

profile of v0, /device:TPU:0, one launch (start us, length us, event | category | flops | bytes accessed | tf_op | source)
XLA Modules:
  0.0 274.0 jit_solution(15575906817718074861)
XLA Ops:
  7.2 0.9 slice_bitcast_fusion.1
  9.9 7.3 %all-to-all-start.2 = ((s32[8,1,2]{2,1,0:T(1,128)}), s32[8,1,2]{2,1,0:T(1,128)S(1)}, u32[]{:S(2)}, u32[]{:S(2)}) async-start(s32[8,1,2]{2,1,0:T(1,128)} %bitcast.18), calls=%async_computation.2 | async-start | bytes 8192 | tf_op jit(solution)/shard_map/all_to_all | solution.py:50
  17.2 2.5 convolution_convert_fusion.3
  19.7 2.2 reshape.166
  21.9 1.5 copy.117
  23.6 5.8 %all-to-all-start.1 = ((bf16[8,2,64,375]{3,1,2,0:T(2,128)(2,1)}), bf16[8,2,64,375]{3,1,2,0:T(2,128)(2,1)S(1)}, u32[]{:S(2)}, u32[]{:S(2)}) async-start(bf16[8,2,64,375]{3,1,2,0:T(2,128)(2,1)} %copy.117), calls=%async_computation.1 | async-start | bytes 1572864 | tf_op jit(solution)/shard_map/all_to_all | solution.py:49
  29.5 19.6 %all-to-all-done.1 = bf16[8,2,64,375]{3,1,2,0:T(2,128)(2,1)S(1)} async-done(((bf16[8,2,64,375]{3,1,2,0:T(2,128)(2,1)}), bf16[8,2,64,375]{3,1,2,0:T(2,128)(2,1)S(1)}, u32[]{:S(2)}, u32[]{:S(2)}) %all-to-all-start.1) | async-done | bytes 768032 | tf_op jit(solution)/shard_map/all_to_all | solution.py:49
  49.2 5.0 %fusion = f32[8,2,64,1500,1]{3,2,4,1,0:T(8,128)} fusion(bf16[2,375,1500,1,1]{2,0,1,4,3:T(2,128)(2,1)S(1)} %bitcast.72, bf16[8,2,2]{2,1,0:T(2,128)(2,1)S(1)} %compare_convert_fusion, bf16[8,2,64,375]{3,2,1,0:T(8,128)(2,1)S(1)} %copy.118), kind=kOutput, calls=%fused_computation | convolution fusion | flops 2304768000 | bytes 9162064 | tf_op jit(solution)/shard_map/ncsig,sgh->hnci/dot_general | solution.py:54
  54.2 6.5 %copy.123 = f32[1500,8,128]{2,1,0:T(8,128)} copy(f32[1500,8,128]{0,2,1:T(8,128)} %bitcast.73) | data formatting | bytes 12288000 | tf_op jit(solution)/shard_map/reshape | solution.py:58
  61.4 26.1 %all-gather = s32[8,16,3]{1,2,0:T(4,128)S(1)} all-gather(s32[1,16,3]{1,2,0:T(4,128)S(1)} %bitcast.81), channel_id=1, replica_groups=mesh['ka'=8,'ga'=4] {'ka'}, dimensions={0}, use_global_device_ids=true | all-gather | bytes 1728 | tf_op jit(solution)/shard_map/all_gather | solution.py:68
  88.5 1.0 copy.111
  89.6 3.5 %all-to-all-start = ((bf16[8,2,64,375]{3,2,1,0:T(8,128)(2,1)}), bf16[8,2,64,375]{3,2,1,0:T(8,128)(2,1)S(1)}, u32[]{:S(2)}, u32[]{:S(2)}) async-start(bf16[8,2,64,375]{3,2,1,0:T(8,128)(2,1)} %copy.111), calls=%async_computation | async-start | bytes 1572864 | tf_op jit(solution)/shard_map/all_to_all | solution.py:87
  93.6 1.0 copy.128
  94.6 13.4 %all-to-all-done = bf16[8,2,64,375]{3,2,1,0:T(8,128)(2,1)S(1)} async-done(((bf16[8,2,64,375]{3,2,1,0:T(8,128)(2,1)}), bf16[8,2,64,375]{3,2,1,0:T(8,128)(2,1)S(1)}, u32[]{:S(2)}, u32[]{:S(2)}) %all-to-all-start) | async-done | bytes 768032 | tf_op jit(solution)/shard_map/all_to_all | solution.py:87
  108.0 4.2 %all-to-all-start.4 = ((bf16[8,2,64,375]{3,2,1,0:T(8,128)(2,1)}), bf16[8,2,64,375]{3,2,1,0:T(8,128)(2,1)}, u32[]{:S(2)}, u32[]{:S(2)}) async-start(bf16[8,2,64,375]{3,2,1,0:T(8,128)(2,1)} %copy.128), calls=%async_computation.4 | async-start | bytes 1572864 | tf_op jit(solution)/shard_map/all_to_all | solution.py:86
  112.2 5.5 %reduce-scatter.4.cloned.1.call-done = f32[375,8,128]{2,1,0:T(8,128)} async-done(((f32[1500,8,128]{2,1,0:T(8,128)}), f32[375,8,128]{2,1,0:T(8,128)}) %reduce-scatter.4.cloned.1.call-update) | async-done | bytes 1536016
  117.7 1.5 convert_element_type.77
  119.1 1.0 copy.124
  120.1 9.4 %all-to-all-done.4 = bf16[8,2,64,375]{3,2,1,0:T(8,128)(2,1)} async-done(((bf16[8,2,64,375]{3,2,1,0:T(8,128)(2,1)}), bf16[8,2,64,375]{3,2,1,0:T(8,128)(2,1)}, u32[]{:S(2)}, u32[]{:S(2)}) %all-to-all-start.4) | async-done | bytes 768032 | tf_op jit(solution)/shard_map/all_to_all | solution.py:86
  129.5 4.2 %all-to-all-start.3 = ((bf16[375,8,128]{2,0,1:T(8,128)(2,1)}), bf16[375,8,128]{2,0,1:T(8,128)(2,1)}, u32[]{:S(2)}, u32[]{:S(2)}) async-start(bf16[375,8,128]{2,0,1:T(8,128)(2,1)} %copy.124), calls=%async_computation.3 | async-start | bytes 1540096 | tf_op jit(solution)/shard_map/all_to_all | solution.py:63
  135.0 2.6 convolution_convert_fusion
  137.7 2.3 fusion.6
  140.0 12.0 %all-to-all-done.3 = bf16[375,8,128]{2,0,1:T(8,128)(2,1)} async-done(((bf16[375,8,128]{2,0,1:T(8,128)(2,1)}), bf16[375,8,128]{2,0,1:T(8,128)(2,1)}, u32[]{:S(2)}, u32[]{:S(2)}) %all-to-all-start.3) | async-done | bytes 768032 | tf_op jit(solution)/shard_map/all_to_all | solution.py:63
  152.0 1.5 copy.125
  154.7 1.2 convolution_subtract_fusion
  156.0 32.5 %all-reduce.5.cloned.1.call-done = f32[16,64,64]{2,1,0:T(8,128)} async-done(((f32[16,64,64]{2,1,0:T(8,128)}), f32[16,64,64]{2,1,0:T(8,128)}) %all-reduce.5.cloned.1.call-update) | async-done | bytes 262160 | tf_op jit(solution)/shard_map/psum | solution.py:110
  188.5 1.3 copy.132
  189.8 0.9 reshape.171
  190.7 2.2 fusion.37
  194.3 0.9 reshape.170
  195.1 70.8 %all-reduce.7.cloned.1.call-done = f32[32,4096]{1,0:T(8,128)} async-done(((f32[32,4096]{1,0:T(8,128)}), f32[32,4096]{1,0:T(8,128)}) %all-reduce.7.cloned.1.call-update) | async-done | bytes 524304
  265.9 1.5 constant_dynamic-slice_fusion
  (50 shorter events, 7.6 us)
Async XLA Ops:
  7.2 42.0 %copy-start = (bf16[2,375,1500]{2,0,1:T(2,128)(2,1)S(1)}, bf16[2,375,1500]{2,0,1:T(2,128)(2,1)}, u32[]{:S(2)}) copy-start(bf16[2,375,1500]{2,0,1:T(2,128)(2,1)} %param.11) | copy-start | bytes 6750004
  9.9 13.7 %all-to-all-start.2 = ((s32[8,1,2]{2,1,0:T(1,128)}), s32[8,1,2]{2,1,0:T(1,128)S(1)}, u32[]{:S(2)}, u32[]{:S(2)}) async-start(s32[8,1,2]{2,1,0:T(1,128)} %bitcast.18), calls=%async_computation.2 | async-start | bytes 8192 | tf_op jit(solution)/shard_map/all_to_all | solution.py:50
  23.6 25.5 %all-to-all-start.1 = ((bf16[8,2,64,375]{3,1,2,0:T(2,128)(2,1)}), bf16[8,2,64,375]{3,1,2,0:T(2,128)(2,1)S(1)}, u32[]{:S(2)}, u32[]{:S(2)}) async-start(bf16[8,2,64,375]{3,1,2,0:T(2,128)(2,1)} %copy.117), calls=%async_computation.1 | async-start | bytes 1572864 | tf_op jit(solution)/shard_map/all_to_all | solution.py:49
  29.4 88.3 %reduce-scatter.4.cloned.1.call-start = ((), (), s32[]{:S(2)}) async-start(), calls=%async_computation.8 | async-start | bytes 7680000
  60.7 0.7 copy-start.6
  60.7 27.4 %copy-start.4 = (bf16[4,64,375]{2,1,0:T(8,128)(2,1)S(1)}, bf16[4,64,375]{2,1,0:T(8,128)(2,1)}, u32[]{:S(2)}) copy-start(bf16[4,64,375]{2,1,0:T(8,128)(2,1)} %param.9) | copy-start | bytes 576004
  88.5 4.6 %copy-start.5 = (bf16[4,64,375]{2,1,0:T(8,128)(2,1)S(1)}, bf16[4,64,375]{2,1,0:T(8,128)(2,1)}, u32[]{:S(2)}) copy-start(bf16[4,64,375]{2,1,0:T(8,128)(2,1)} %param.8) | copy-start | bytes 576004
  89.6 18.4 %all-to-all-start = ((bf16[8,2,64,375]{3,2,1,0:T(8,128)(2,1)}), bf16[8,2,64,375]{3,2,1,0:T(8,128)(2,1)S(1)}, u32[]{:S(2)}, u32[]{:S(2)}) async-start(bf16[8,2,64,375]{3,2,1,0:T(8,128)(2,1)} %copy.111), calls=%async_computation | async-start | bytes 1572864 | tf_op jit(solution)/shard_map/all_to_all | solution.py:87
  108.0 21.6 %all-to-all-start.4 = ((bf16[8,2,64,375]{3,2,1,0:T(8,128)(2,1)}), bf16[8,2,64,375]{3,2,1,0:T(8,128)(2,1)}, u32[]{:S(2)}, u32[]{:S(2)}) async-start(bf16[8,2,64,375]{3,2,1,0:T(8,128)(2,1)} %copy.128), calls=%async_computation.4 | async-start | bytes 1572864 | tf_op jit(solution)/shard_map/all_to_all | solution.py:86
  119.1 14.9 %copy-start.7 = (f32[375]{0:T(512)S(1)}, f32[375]{0:T(512)}, u32[]{:S(2)}) copy-start(f32[375]{0:T(512)} %param.10) | copy-start | bytes 4504
  129.5 22.4 %all-to-all-start.3 = ((bf16[375,8,128]{2,0,1:T(8,128)(2,1)}), bf16[375,8,128]{2,0,1:T(8,128)(2,1)}, u32[]{:S(2)}, u32[]{:S(2)}) async-start(bf16[375,8,128]{2,0,1:T(8,128)(2,1)} %copy.124), calls=%async_computation.3 | async-start | bytes 1540096 | tf_op jit(solution)/shard_map/all_to_all | solution.py:63
  133.7 54.8 %all-reduce.5.cloned.1.call-start = ((), (), s32[]{:S(2)}) async-start(), calls=%async_computation.6 | async-start | bytes 1048576 | tf_op jit(solution)/shard_map/psum | solution.py:110
  153.5 1.1 copy-start.1
  153.5 1.3 copy-start.3
  156.0 109.9 %all-reduce.7.cloned.1.call-start = ((), (), s32[]{:S(2)}) async-start(), calls=%async_computation.7 | async-start | bytes 1048576
  188.5 4.5 %copy-start.8 = (u32[32]{0:T(128)S(1)}, u32[32]{0:T(128)}, u32[]{:S(2)}) copy-start(u32[32]{0:T(128)} %constant.69) | copy-start | bytes 388
  188.5 5.7 %copy-start.2 = (f32[16,64,64]{2,1,0:T(8,128)S(1)}, f32[16,64,64]{2,1,0:T(8,128)}, u32[]{:S(2)}) copy-start(f32[16,64,64]{2,1,0:T(8,128)} %all-reduce.5.cloned.1.call-done) | copy-start | bytes 786436
Sparse Core Ops, SparseCore 0:
  60.9 56.7 reduce-scatter.3
  156.1 32.3 all-reduce.4
  193.1 72.7 all-reduce.6
where the time goes:
time: 275 us; the launch traced here: 274 us
  waiting for transfers between devices  163 us (59%)
  blocking collectives  26.1 us (9%)
  starting transfers between devices  25.2 us (9%)
  local copies, waits for them, and re-layouts  22.1 us (8%)
  matrix products  18.5 us (7%)
  between operations  14.6 us (5%)
  other arithmetic  4.08 us (1%)
    unnamed x5, waiting for transfers between devices  76.3 us
    psum x1, waiting for transfers between devices, per_device(): kernel_block = lax.psum(2.0 * exchange_term - direct, 'ga')  32.5 us
    all_gather x1, blocking collectives, per_device(): lax.all_gather(pairs, 'ka', axis=0, tiled=True).reshape(n_ka, pair_rows, 3)  26.1 us
    all_to_all x1, waiting for transfers between devices, per_device(): lax.all_to_all(send_x, 'ka', split_axis=0, concat_axis=0, tiled=True)  19.6 us
    all_to_all x1, waiting for transfers between devices, per_device(): lax.all_to_all(send_p, 'ka', split_axis=0, concat_axis=0, tiled=True)  13.4 us
    all_to_all x1, waiting for transfers between devices, per_device(): lax.all_to_all(half_rows, 'ka', split_axis=1, concat_axis=1, tiled=True)  12 us
    all_to_all x1, waiting for transfers between devices, per_device(): lax.all_to_all(send_y, 'ka', split_axis=0, concat_axis=0, tiled=True)  9.42 us
    all_to_all x1, starting transfers between devices, per_device(): lax.all_to_all(send_q, 'ka', split_axis=0, concat_axis=0, tiled=True)  7.31 us
  transfers between devices with their start and end apart: 8, of which 8 were waited for; matrix products, arithmetic and copies ran while one was open for 7% of the time, Pallas kernels for 0%

commit v1 on v0

v1 whole, which is shorter than its diff:
```python
import functools
import jax
import jax.numpy as jnp
from jax import lax
from jax.experimental import pallas as pl
from jax.experimental.pallas import tpu as pltpu
from jax.sharding import PartitionSpec as P

CAPQ = 2
F32 = jnp.float32
BF16 = jnp.bfloat16
VM = pl.BlockSpec(memory_space=pltpu.VMEM)
SM = pl.BlockSpec(memory_space=pltpu.SMEM)
LIMIT = 66000000


class Gather:
    def __init__(self, n, src, out, send, recv):
        self.n, self.nz = n, n // 2
        self.me = lax.axis_index("ka")
        self.z, self.y = self.me // 2, self.me % 2
        self.src, self.out, self.send, self.recv = src, out, send, recv
        self.size = src.shape[0]
        self.half = self.size // 2

    def copy(self, zz, yy, half, way, own=False):
        block = self.out.at[pl.ds((zz * 2 + yy) * self.size + half * self.half, self.half)]
        source = self.src.at[pl.ds(half * self.half, self.half)] if own else block
        index = (zz * 2 + yy) * 2 + half
        if way == 2:
            target = self.z * 2 + 1 - self.y
        else:
            step = 1 if way == 0 else -1
            target = (self.z + step) * 2 + self.y
        return pltpu.make_async_remote_copy(
            src_ref=source,
            dst_ref=block,
            send_sem=self.send.at[way * 2 * self.n + index],
            recv_sem=self.recv.at[index],
            device_id={"ka": target},
            device_id_type=pl.DeviceIdType.MESH,
        )

    def chain(self, zz, yy, half, act, ways=(0, 1), own=False):
        for way in ways:
            free = self.z < self.nz - 1 if way == 0 else self.z > 0

            @pl.when(free)
            def _(way=way):
                act(self.copy(zz, yy, half, way, own))

    def first(self):
        start = lambda c: c.start()
        self.copy(self.z, self.y, 1, 2, True).start()
        self.chain(self.z, self.y, 0, start, own=True)
        self.chain(self.z, self.y, 1, start, own=True)
        self.copy(self.z, self.y, 0, 2, True).start()
        self.out[pl.ds(self.me * self.size, self.size)] = self.src[...]

    def second(self):
        start = lambda c: c.start()
        self.copy(self.z, 1 - self.y, 1, 2).wait_recv()
        self.chain(self.z, 1 - self.y, 1, start)

    def hop(self, h):
        start = lambda c: c.start()
        for way in (0, 1):
            zz = self.z - h if way == 0 else self.z + h
            there = zz >= 0 if way == 0 else zz < self.nz

            @pl.when(there)
            def _(zz=zz, way=way):
                for yy, half in ((self.y, 0), (self.y, 1), (1 - self.y, 1)):
                    self.copy(zz, yy, half, 2).wait_recv()
                    self.chain(zz, yy, half, start, (way,))
                    if half == 0:
                        self.copy(zz, yy, 0, 2).start()

    def finish(self):
        done = lambda c: c.wait_send()
        self.copy(self.z, self.y, 1, 2, True).wait_send()
        for half in (0, 1):
            self.chain(self.z, self.y, half, done, own=True)
        self.copy(self.z, self.y, 0, 2, True).wait_send()
        self.chain(self.z, 1 - self.y, 1, done)
        self.copy(self.z, 1 - self.y, 0, 2).wait_recv()

        def tail(h, carry):
            for way in (0, 1):
                zz = self.z - h if way == 0 else self.z + h
                there = zz >= 0 if way == 0 else zz < self.nz

                @pl.when(there)
                def _(zz=zz, way=way):
                    for yy, half in ((self.y, 0), (self.y, 1), (1 - self.y, 1)):
                        self.chain(zz, yy, half, done, (way,))
                    self.copy(zz, self.y, 0, 2).wait_send()
                    self.copy(zz, 1 - self.y, 0, 2).wait_recv()

            return carry

        lax.fori_loop(1, self.nz, tail, 0)


def run_gathers(gathers, between=None):
    for g in gathers:
        g.first()
    for g in gathers:
        g.second()
    if between is not None:
        between()

    def body(h, carry):
        for g in gathers:
            g.hop(h)
        return carry

    lax.fori_loop(1, gathers[0].nz, body, 0)
    for g in gathers:
        g.finish()


def greet(n, ka_too, ga_too):
    barrier = pltpu.get_barrier_semaphore()
    me = lax.axis_index("ka")
    z, y = me // 2, me % 2
    nz = n // 2
    targets = []
    if ka_too:
        targets += [{"ka": lax.rem(z + 1, nz) * 2 + y}, {"ka": lax.rem(z + nz - 1, nz) * 2 + y}]
        targets += [{"ka": z * 2 + 1 - y}]
    if ga_too:
        g = lax.axis_index("ga")
        n_ga = lax.axis_size("ga")
        targets += [{"ga": lax.rem(g + i, n_ga)} for i in range(1, n_ga)]
    for t in targets:
        pl.semaphore_signal(barrier, inc=1, device_id=t, device_id_type=pl.DeviceIdType.MESH)
    pl.semaphore_wait(barrier, len(targets))


def gather_sems(n):
    return [pltpu.SemaphoreType.DMA((6 * n,)), pltpu.SemaphoreType.DMA((2 * n,))]


def params(collective_id):
    return pltpu.CompilerParams(
        collective_id=collective_id, has_side_effects=True, vmem_limit_bytes=LIMIT
    )


def first_kernel(n, x_ref, l_ref, xo_ref, lo_ref, xs, xr, ls, lr):
    greet(n, True, False)
    run_gathers([Gather(n, l_ref, lo_ref, ls, lr), Gather(n, x_ref, xo_ref, xs, xr)])


def half_kernel(n, rows, q_slots, list_ref, qs_ref, x_ref, w_ref, o_ref, k_ref, k2_ref, at_ref, w_at, count):
    me = lax.axis_index("ka")
    slots = n * CAPQ

    def clear(s, c):
        k_ref[s] = 0
        k2_ref[s] = 0
        w_at[s] = 0
        return c

    lax.fori_loop(0, slots, clear, 0)

    def source(a, c):
        def zero(o, c):
            count[o] = 0
            return c

        lax.fori_loop(0, n, zero, 0)

        def pair(j, c):
            r = a * rows + j
            slot = qs_ref[list_ref[r * 3 + 2]]
            owner = slot // q_slots
            rank = count[owner]
            count[owner] = rank + 1
            at_ref[r] = owner * CAPQ + rank

            @pl.when(owner == me)
            def _():
                s = a * CAPQ + rank
                k_ref[s] = list_ref[r * 3]
                k2_ref[s] = list_ref[r * 3 + 1]
                w_at[s] = slot % q_slots

            return c

        return lax.fori_loop(0, rows, pair, c)

    lax.fori_loop(0, n, source, 0)
    n_ga, g = o_ref.shape[0], o_ref.shape[3]

    def multiply(s, c):
        v = jnp.dot(x_ref[k_ref[s]], w_ref[w_at[s]], preferred_element_type=F32)
        for i in range(n_ga):
            o_ref[i, s] = v[:, i * g : (i + 1) * g].astype(o_ref.dtype)
        return c

    lax.fori_loop(0, slots, multiply, 0)


def reduce_two(part, out, recv1, tsend, recv2, s1, r1, s2, r2, pieces):
    g = lax.axis_index("ga")
    x, c = g // 2, g % 2
    per = part.shape[1] // pieces
    there, here = 1 - x, x

    def one(t, xx, i):
        rows = pl.ds(i * per, per)
        return pltpu.make_async_remote_copy(
            src_ref=part.at[xx * 2 + 1 - c, rows],
            dst_ref=recv1.at[xx, rows],
            send_sem=s1.at[t * pieces + i],
            recv_sem=r1.at[t * pieces + i],
            device_id={"ga": x * 2 + 1 - c},
            device_id_type=pl.DeviceIdType.MESH,
        )

    def two(i):
        rows = pl.ds(i * per, per)
        return pltpu.make_async_remote_copy(
            src_ref=tsend.at[rows],
            dst_ref=recv2.at[rows],
            send_sem=s2.at[i],
            recv_sem=r2.at[i],
            device_id={"ga": there * 2 + c},
            device_id_type=pl.DeviceIdType.MESH,
        )

    def begin():
        for i in range(pieces):
            one(0, there, i).start()
        for i in range(pieces):
            one(1, here, i).start()

    def middle():
        for i in range(pieces):
            rows = pl.ds(i * per, per)
            one(0, there, i).wait_recv()
            v = part[there * 2 + c, rows].astype(F32) + recv1[there, rows].astype(F32)
            tsend[rows] = v.astype(tsend.dtype)
            two(i).start()

    def end():
        for i in range(pieces):
            rows = pl.ds(i * per, per)
            one(1, here, i).wait_recv()
            two(i).wait_recv()
            v = part[here * 2 + c, rows].astype(F32) + recv1[here, rows].astype(F32)
            out[rows] = (v + recv2[rows].astype(F32)).astype(out.dtype)
        for i in range(pieces):
            one(0, there, i).wait_send()
            one(1, here, i).wait_send()
            two(i).wait_send()

    return begin, middle, end


def second_kernel(n, pieces, part, y_ref, p_ref, half_ref, yo_ref, po_ref, recv1, tsend, recv2,
                  s1, r1, s2, r2, ys, yr, ps, pr):
    greet(n, True, True)
    begin, middle, end = reduce_two(part, half_ref, recv1, tsend, recv2, s1, r1, s2, r2, pieces)
    begin()
    run_gathers([Gather(n, y_ref, yo_ref, ys, yr), Gather(n, p_ref, po_ref, ps, pr)], middle)
    end()


def block_kernel(n, k_ref, k2_ref, half_ref, y_ref, p_ref, v_ref, o_ref):
    n_ga, quarter = o_ref.shape[0], o_ref.shape[2]
    dims = (((1,), (1,)), ((), ()))

    def source(a, carry):
        both = []
        for c in range(CAPQ):
            s = a * CAPQ + c
            k, k2 = k_ref[s], k2_ref[s]
            direct = lax.dot_general(half_ref[s], y_ref[k2], dims, preferred_element_type=F32)
            weighted = p_ref[k].astype(F32) * v_ref[...]
            high = weighted.astype(BF16)
            low = (weighted - high.astype(F32)).astype(BF16)
            other = p_ref[k2]
            term = lax.dot_general(high, other, dims, preferred_element_type=F32)
            term += lax.dot_general(low, other, dims, preferred_element_type=F32)
            both.append(2.0 * term - direct)
        v = jnp.concatenate(both, axis=1)
        for i in range(n_ga):
            o_ref[i, a] = v[i * quarter : (i + 1) * quarter]
        return carry

    lax.fori_loop(0, n, source, 0)


def third_kernel(n, part, all_ref, own, recv1, tsend, recv2, s1, r1, s2, r2, gs, gr):
    greet(n, True, True)
    begin, middle, end = reduce_two(part, own, recv1, tsend, recv2, s1, r1, s2, r2, 1)
    begin()
    middle()
    end()
    run_gathers([Gather(n, own, all_ref, gs, gr)])


def select_kernel(n, rows, per_dev, list_ref, at_ref, all_ref, o_ref, acc):
    me = lax.axis_index("ka")
    nt = all_ref.shape[2] // CAPQ

    def tile(a, j):
        at = at_ref[a * rows + j]
        both = all_ref[(at // CAPQ) * n + a]
        return jnp.where(at % CAPQ == 0, both[:, :nt], both[:, nt:])

    for j in range(rows // 2):
        o_ref[j] = jnp.concatenate([tile(me, j), tile(me, j + rows // 2)], axis=1)
    acc[...] = jnp.zeros_like(acc)

    def pair(r, c):
        second = list_ref[r * 3 + 1] - me * per_dev

        @pl.when(jnp.logical_and(second >= 0, second < per_dev))
        def _():
            a = r // rows
            acc[second] = acc[second] + tile(a, r - a * rows)

        return c

    lax.fori_loop(0, n * rows, pair, 0)
    for k in range(per_dev // 2):
        o_ref[rows // 2 + k] = jnp.concatenate([acc[k], acc[k + per_dev // 2]], axis=1)


def fourth_kernel(n, src, out, send, recv):
    greet(n, False, True)
    g = lax.axis_index("ga")
    n_ga = out.shape[0]
    copies = [
        pltpu.make_async_remote_copy(
            src_ref=src,
            dst_ref=out.at[g],
            send_sem=send.at[i],
            recv_sem=recv.at[i],
            device_id={"ga": lax.rem(g + i, n_ga)},
            device_id_type=pl.DeviceIdType.MESH,
        )
        for i in range(1, n_ga)
    ]
    for c in copies:
        c.start()
    out[g] = src[...]
    for c in copies:
        c.wait()


def per_device(x_dens, y_dens, p_dens, coulomb, screened, pairs, q_slot):
    n = lax.axis_size("ka")
    n_ga = lax.axis_size("ga")
    per_dev, nt, g = x_dens.shape
    q_slots = screened.shape[0]
    rows = pairs.shape[0]
    slots = n * CAPQ
    shape = jax.ShapeDtypeStruct
    listed = jnp.pad(pairs, ((0, 0), (0, 128 - pairs.shape[1]))).reshape(2, rows // 2, 128)
    x_all, listed = pl.pallas_call(
        functools.partial(first_kernel, n),
        out_shape=[shape((n * per_dev, nt, g), BF16), shape((n * 2, rows // 2, 128), jnp.int32)],
        in_specs=[VM, VM],
        out_specs=[VM, VM],
        scratch_shapes=gather_sems(n) + gather_sems(n),
        compiler_params=params(0),
        name="gather_x",
    )(x_dens, listed)
    listed = listed.reshape(n * rows, 128)[:, :3].reshape(n * rows * 3)
    wide = F32 if slots * nt <= 2048 else BF16
    ints = lambda m: shape((m,), jnp.int32)
    part, k_at, k2_at, at = pl.pallas_call(
        functools.partial(half_kernel, n, rows, q_slots),
        out_shape=[shape((n_ga, slots, nt, g), wide), ints(slots), ints(slots), ints(n * rows)],
        in_specs=[SM, SM, VM, VM],
        out_specs=[VM, SM, SM, SM],
        scratch_shapes=[pltpu.SMEM((slots,), jnp.int32), pltpu.SMEM((n,), jnp.int32)],
        compiler_params=pltpu.CompilerParams(vmem_limit_bytes=LIMIT),
        name="half",
    )(listed, q_slot, x_all, screened)
    pieces = 4
    half, y_all, p_all = pl.pallas_call(
        functools.partial(second_kernel, n, pieces),
        out_shape=[shape((slots, nt, g), BF16)] + [shape((n * per_dev, nt, g), BF16)] * 2,
        in_specs=[VM, VM, VM],
        out_specs=[VM, VM, VM],
        scratch_shapes=[
            pltpu.VMEM((2, slots, nt, g), wide),
            pltpu.VMEM((slots, nt, g), BF16),
            pltpu.VMEM((slots, nt, g), BF16),
            pltpu.SemaphoreType.DMA((2 * pieces,)),
            pltpu.SemaphoreType.DMA((2 * pieces,)),
            pltpu.SemaphoreType.DMA((pieces,)),
            pltpu.SemaphoreType.DMA((pieces,)),
        ]
        + gather_sems(n)
        + gather_sems(n),
        compiler_params=params(1),
        name="reduce_gather",
    )(part, y_dens, p_dens)
    quarter = nt // n_ga
    block = pl.pallas_call(
        functools.partial(block_kernel, n),
        out_shape=shape((n_ga, n, quarter, CAPQ * nt), F32),
        in_specs=[SM, SM, VM, VM, VM, VM],
        out_specs=VM,
        compiler_params=pltpu.CompilerParams(vmem_limit_bytes=LIMIT),
        name="block",
    )(k_at, k2_at, half, y_all, p_all, coulomb.reshape(1, g))
    line = (n, quarter, CAPQ * nt)
    everything = pl.pallas_call(
        functools.partial(third_kernel, n),
        out_shape=shape((n * n, quarter, CAPQ * nt), F32),
        in_specs=[VM],
        out_specs=VM,
        scratch_shapes=[
            pltpu.VMEM(line, F32),
            pltpu.VMEM((2,) + line, F32),
            pltpu.VMEM(line, F32),
            pltpu.VMEM(line, F32),
        ]
        + [pltpu.SemaphoreType.DMA((2,))] * 4
        + gather_sems(n),
        compiler_params=params(2),
        name="reduce_blocks",
    )(block)
    lines = rows // 2 + per_dev // 2
    mine = pl.pallas_call(
        functools.partial(select_kernel, n, rows, per_dev),
        out_shape=shape((lines, quarter, 2 * nt), F32),
        in_specs=[SM, SM, VM],
        out_specs=VM,
        scratch_shapes=[pltpu.VMEM((per_dev, quarter, nt), F32)],
        compiler_params=pltpu.CompilerParams(vmem_limit_bytes=LIMIT),
        name="select",
    )(listed, at, everything)
    full = pl.pallas_call(
        functools.partial(fourth_kernel, n),
        out_shape=shape((n_ga, lines, quarter, 2 * nt), F32),
        in_specs=[VM],
        out_specs=VM,
        scratch_shapes=[pltpu.SemaphoreType.DMA((n_ga,))] * 2,
        compiler_params=params(3),
        name="gather_out",
    )(mine)
    split = lambda v: jnp.concatenate([v[..., :nt], v[..., nt:]], axis=1)
    blocks = split(full[:, : rows // 2]).transpose(1, 0, 2, 3).reshape(rows, nt * nt)
    mirrored = split(full[:, rows // 2 :]).transpose(1, 3, 0, 2).reshape(per_dev, nt * nt)
    return (blocks, mirrored)


def solution(mesh):
    in_specs = (
        P("ka", None, "ga"),
        P("ka", None, "ga"),
        P("ka", None, "ga"),
        P("ga"),
        P("ka", "ga", None),
        P("ka", None),
        P(),
    )
    out_specs = (P("ka", None), P("ka", None))
    return jax.shard_map(
        per_device, mesh=mesh, in_specs=in_specs, out_specs=out_specs, check_vma=False
    )
```

time: 275 us -> 147 us (0.53)
  waiting for transfers between devices: 163 us -> 0 us
  Pallas kernels: 0 us -> 134 us
  blocking collectives: 26.1 us -> 0 us
  starting transfers between devices: 25.2 us -> 0 us
  matrix products: 18.5 us -> 0 us
  between operations: 14.6 us -> 0.72 us
  local copies, waits for them, and re-layouts: 22.1 us -> 11.3 us
  other arithmetic: 4.08 us -> 0.06 us
    pallas_call x0 -> x7, Pallas kernels: none -> 134 us  [the longest x1 48.1 us: per_device(): pl.pallas_call(functools.partial(second_kernel, n, pieces), out_shape=[sh...]
    unnamed x5 -> x0, waiting for transfers between devices: 76.3 us -> none
    all_to_all x5 -> x0, waiting for transfers between devices: 54.6 us -> none  [the longest x1 19.6 us: per_device(): lax.all_to_all(send_x, 'ka', split_axis=0, concat_axis=0, tiled=True)]
    psum x1 -> x0, waiting for transfers between devices: 32.5 us -> none  [per_device(): kernel_block = lax.psum(2.0 * exchange_term - direct, 'ga')]
    all_gather x1 -> x0, blocking collectives: 26.1 us -> none  [per_device(): lax.all_gather(pairs, 'ka', axis=0, tiled=True).reshape(n_ka, pair_rows, 3)]
    all_to_all x5 -> x0, starting transfers between devices: 25 us -> none  [the longest x1 7.31 us: per_device(): lax.all_to_all(send_q, 'ka', split_axis=0, concat_axis=0, tiled=True)]
    dot_general x12 -> x0, matrix products: 18.5 us -> none  [the longest x1 4.99 us: per_device(): jnp.einsum('ncsig,sgh->hnci', stacked, screened, preferred_element_type=j...]
    reshape x5, local copies, waits for them, and re-layouts: 11.9 us -> 4.78 us  [the longest x1 1.62 us: per_device(): listed = listed.reshape(n * rows, 128)[:, :3].reshape(n * rows * 3)]
  transfers between devices with their start and end apart: 8 -> 0, of which waited for: 8 -> 0; matrix products, arithmetic and copies ran while one was open for 7% -> 0% of each run, Pallas kernels for 0% -> 0%
where the time goes in v1:
time: 147 us; the launch traced here: 146 us
  Pallas kernels  134 us (91%)
  local copies, waits for them, and re-layouts  11.3 us (8%)
    pallas_call x1, Pallas kernels, per_device(): pl.pallas_call(functools.partial(second_kernel, n, pieces), out_shape=[sh...  48.1 us
    pallas_call x1, Pallas kernels, per_device(): pl.pallas_call(functools.partial(first_kernel, n), out_shape=[shape((n *...  31.7 us
    pallas_call x1, Pallas kernels, per_device(): pl.pallas_call(functools.partial(third_kernel, n), out_shape=shape((n * n...  21.2 us
    pallas_call x1, Pallas kernels, per_device(): pl.pallas_call(functools.partial(half_kernel, n, rows, q_slots), out_shap...  15.6 us
    pallas_call x1, Pallas kernels, per_device(): pl.pallas_call(functools.partial(fourth_kernel, n), out_shape=shape((n_ga...  7.52 us
    pallas_call x1, Pallas kernels, per_device(): pl.pallas_call(functools.partial(block_kernel, n), out_shape=shape((n_ga,...  5.42 us
    pallas_call x1, Pallas kernels, per_device(): pl.pallas_call(functools.partial(select_kernel, n, rows, per_dev), out_sh...  4.36 us
    unnamed x4, local copies, waits for them, and re-layouts  4.06 us

profile of v1, /device:TPU:0, one launch (start us, length us, event | category | flops | bytes accessed | tf_op | source)
XLA Modules:
  0.0 146.0 jit_solution(8717013452129860692)
XLA Ops:
  0.6 0.8 copy.15
  1.4 0.6 pad_bitcast_fusion.l_ref
  2.0 31.7 %gather_x.1 = (bf16[32,64,375]{2,1,0:T(8,128)(2,1)}, s32[16,8,128]{2,1,0:T(8,128)}) custom-call(bf16[4,64,375]{2,1,0:T(8,128)(2,1)} %x_ref.1, s32[2,8,128]{2,1,0:T(8,128)} %pad_bitcast_fusion.l_ref), custom_call_target="tpu_custom_call" | custom-call | tf_op jit(solution)/shard_map/gather_x/pallas_call | solution.py:365
  33.7 1.6 %reshape.24.list_ref = s32[384]{0:T(512)} reshape(s32[128,3]{1,0:T(8,128)} %bitcast.10) | data formatting | bytes 3072 | tf_op jit(solution)/shard_map/reshape | solution.py:374
  35.3 3.3 %copy.12.w_ref = bf16[2,375,1500]{2,1,0:T(8,128)(2,1)} copy(bf16[2,375,1500]{2,0,1:T(2,128)(2,1)} %param.11) | data formatting | bytes 4500000 | tf_op args[4]
  38.6 15.6 %half.1 = (f32[4,16,64,375]{3,2,1,0:T(8,128)}, s32[16]{0:T(128)}, s32[16]{0:T(128)}, s32[128]{0:T(128)}) custom-call(s32[384]{0:T(512)} %reshape.24.list_ref, s32[16]{0:T(128)} %qs_ref.1, bf16[32,64,375]{2,1,0:T(8,128)(2,1)} %get-tuple-element.12.x_ref, bf16[2,375,1500]{2,1,0:T(8,128)(2,1)} %copy.12.w_ref), custom_call_target="tpu_custom_call" | custom-call | tf_op jit(solution)/shard_map/half/pallas_call | solution.py:377
  54.2 0.0 copy-start
  54.2 48.1 %reduce_gather.1 = (bf16[16,64,375]{2,1,0:T(8,128)(2,1)}, bf16[32,64,375]{2,1,0:T(8,128)(2,1)}, bf16[32,64,375]{2,1,0:T(8,128)(2,1)}) custom-call(f32[4,16,64,375]{3,2,1,0:T(8,128)} %get-tuple-element.16.part, bf16[4,64,375]{2,1,0:T(8,128)(2,1)} %y_ref.1, bf16[4,64,375]{2,1,0:T(8,128)(2,1)} %p_ref.1), custom_call_target="tpu_custom_call" | custom-call | tf_op jit(solution)/shard_map/reduce_gather/pallas_call | solution.py:387
  102.4 0.0 copy-done
  102.4 0.6 reshape.25.v_ref
  103.0 5.4 %block.1.part = f32[4,8,16,128]{3,2,1,0:T(8,128)} custom-call(s32[16]{0:T(128)} %get-tuple-element.14.k_ref, s32[16]{0:T(128)} %get-tuple-element.15.k2_ref, bf16[16,64,375]{2,1,0:T(8,128)(2,1)} %get-tuple-element.17.half_ref, bf16[32,64,375]{2,1,0:T(8,128)(2,1)} %get-tuple-element.18.y_ref, bf16[32,64,375]{2,1,0:T(8,128)(2,1)} %get-tuple-element.19.p_ref, ...), custom_call_target="tpu_custom_call" | custom-call | tf_op jit(solution)/shard_map/block/pallas_call | solution.py:407
  108.4 21.2 %reduce_blocks.1.all_ref = f32[64,16,128]{2,1,0:T(8,128)} custom-call(f32[4,8,16,128]{3,2,1,0:T(8,128)} %block.1.part), custom_call_target="tpu_custom_call" | custom-call | tf_op jit(solution)/shard_map/reduce_blocks/pallas_call | solution.py:416
  129.6 4.4 %select.2.src = f32[10,16,128]{2,1,0:T(8,128)} custom-call(s32[384]{0:T(512)} %reshape.24.list_ref, s32[128]{0:T(128)} %get-tuple-element.13.at_ref, f32[64,16,128]{2,1,0:T(8,128)} %reduce_blocks.1.all_ref), custom_call_target="tpu_custom_call" | custom-call | tf_op jit(solution)/shard_map/select/pallas_call | solution.py:433
  133.9 7.5 %gather_out.1 = f32[4,10,16,128]{3,2,1,0:T(8,128)} custom-call(f32[10,16,128]{2,1,0:T(8,128)} %select.2.src), custom_call_target="tpu_custom_call" | custom-call | tf_op jit(solution)/shard_map/gather_out/pallas_call | solution.py:442
  141.5 1.2 fusion.1
  142.8 0.9 reshape.26
  143.6 1.0 fusion
  144.7 0.2 copy.14
  144.9 1.1 reshape.27
  (3 shorter events, 0.1 us)
Async XLA Ops:
  54.2 48.1 %copy-start = (f32[375]{0:T(512)S(1)}, f32[375]{0:T(512)}, u32[]{:S(2)}) copy-start(f32[375]{0:T(512)} %param.10) | copy-start | bytes 4504

commit v2 on v1

--- a/solution.py
+++ b/solution.py
@@ -21,11 +21,12 @@
         self.z, self.y = self.me // 2, self.me % 2
         self.src, self.out, self.send, self.recv = src, out, send, recv
         self.size = src.shape[0]
-        self.half = self.size // 2
+        self.cut = self.size - max(1, self.size // 6)
 
     def copy(self, zz, yy, half, way, own=False):
-        block = self.out.at[pl.ds((zz * 2 + yy) * self.size + half * self.half, self.half)]
-        source = self.src.at[pl.ds(half * self.half, self.half)] if own else block
+        first, length = (self.cut, self.size - self.cut) if half else (0, self.cut)
+        block = self.out.at[pl.ds((zz * 2 + yy) * self.size + first, length)]
+        source = self.src.at[pl.ds(first, length)] if own else block
         index = (zz * 2 + yy) * 2 + half
         if way == 2:
             target = self.z * 2 + 1 - self.y
@@ -120,7 +121,7 @@
         g.finish()
 
 
-def greet(n, ka_too, ga_too):
+def greet(n, ka_too, ga_too, all_ka=False):
     barrier = pltpu.get_barrier_semaphore()
     me = lax.axis_index("ka")
     z, y = me // 2, me % 2
@@ -129,6 +130,8 @@
     if ka_too:
         targets += [{"ka": lax.rem(z + 1, nz) * 2 + y}, {"ka": lax.rem(z + nz - 1, nz) * 2 + y}]
         targets += [{"ka": z * 2 + 1 - y}]
+    if all_ka:
+        targets += [{"ka": lax.rem(me + i, n)} for i in range(1, n)]
     if ga_too:
         g = lax.axis_index("ga")
         n_ga = lax.axis_size("ga")
@@ -159,7 +162,7 @@
 
     def clear(s, c):
         k_ref[s] = 0
-        k2_ref[s] = 0
+        k2_ref[s] = -1
         w_at[s] = 0
         return c
 
@@ -277,7 +280,7 @@
         both = []
         for c in range(CAPQ):
             s = a * CAPQ + c
-            k, k2 = k_ref[s], k2_ref[s]
+            k, k2 = k_ref[s], jnp.maximum(k2_ref[s], 0)
             direct = lax.dot_general(half_ref[s], y_ref[k2], dims, preferred_element_type=F32)
             weighted = p_ref[k].astype(F32) * v_ref[...]
             high = weighted.astype(BF16)
@@ -294,53 +297,73 @@
     lax.fori_loop(0, n, source, 0)
 
 
-def third_kernel(n, part, all_ref, own, recv1, tsend, recv2, s1, r1, s2, r2, gs, gr):
-    greet(n, True, True)
+def tail_kernel(n, rows, per_dev, k2_ref, at_ref, part, out, own, recv1, tsend, recv2, second,
+                outbox, inbox, lines, s1, r1, s2, r2, as_, ar, gs, gr):
+    greet(n, False, True, True)
     begin, middle, end = reduce_two(part, own, recv1, tsend, recv2, s1, r1, s2, r2, 1)
     begin()
+    me = lax.axis_index("ka")
+    g = lax.axis_index("ga")
+    n_ga = out.shape[0]
+    shape = own.shape[1:]
+    nt = shape[1] // CAPQ
+    left = lax.broadcasted_iota(jnp.int32, shape, 1) < nt
+    for a in range(n):
+        second[a] = jnp.where(left, k2_ref[a * CAPQ], k2_ref[a * CAPQ + 1])
     middle()
     end()
-    run_gathers([Gather(n, own, all_ref, gs, gr)])
-
-
-def select_kernel(n, rows, per_dev, list_ref, at_ref, all_ref, o_ref, acc):
-    me = lax.axis_index("ka")
-    nt = all_ref.shape[2] // CAPQ
-
-    def tile(a, j):
-        at = at_ref[a * rows + j]
-        both = all_ref[(at // CAPQ) * n + a]
+    pairs = per_dev // 2
+
+    def summed(k):
+        total = jnp.zeros(shape, F32)
+        for a in range(n):
+            total += jnp.where(second[a] == k, own[a], 0.0)
+        return total[:, :nt] + total[:, nt:]
+
+    def fill(b, carry):
+        outbox[b, 0] = own[b]
+        for i in range(pairs):
+            k = b * per_dev + i
+            outbox[b, 1 + i] = jnp.concatenate([summed(k), summed(k + pairs)], axis=1)
+        return carry
+
+    lax.fori_loop(0, n, fill, 0)
+
+    def cross(i):
+        to = lax.rem(me + i, n)
+        return pltpu.make_async_remote_copy(
+            src_ref=outbox.at[to],
+            dst_ref=inbox.at[me],
+            send_sem=as_.at[i],
+            recv_sem=ar.at[i],
+            device_id={"ka": to},
+            device_id_type=pl.DeviceIdType.MESH,
+        )
+
+    for i in range(1, n):
+        cross(i).start()
+    inbox[me] = outbox[me]
+    for i in range(1, n):
+        cross(i).wait()
+
+    def tile(j):
+        at = at_ref[me * rows + j]
+        both = inbox[at // CAPQ, 0]
         return jnp.where(at % CAPQ == 0, both[:, :nt], both[:, nt:])
 
     for j in range(rows // 2):
-        o_ref[j] = jnp.concatenate([tile(me, j), tile(me, j + rows // 2)], axis=1)
-    acc[...] = jnp.zeros_like(acc)
-
-    def pair(r, c):
-        second = list_ref[r * 3 + 1] - me * per_dev
-
-        @pl.when(jnp.logical_and(second >= 0, second < per_dev))
-        def _():
-            a = r // rows
-            acc[second] = acc[second] + tile(a, r - a * rows)
-
-        return c
-
-    lax.fori_loop(0, n * rows, pair, 0)
-    for k in range(per_dev // 2):
-        o_ref[rows // 2 + k] = jnp.concatenate([acc[k], acc[k + per_dev // 2]], axis=1)
-
-
-def fourth_kernel(n, src, out, send, recv):
-    greet(n, False, True)
-    g = lax.axis_index("ga")
-    n_ga = out.shape[0]
+        lines[j] = jnp.concatenate([tile(j), tile(j + rows // 2)], axis=1)
+    for i in range(pairs):
+        total = inbox[0, 1 + i]
+        for o in range(1, n):
+            total += inbox[o, 1 + i]
+        lines[rows // 2 + i] = total
     copies = [
         pltpu.make_async_remote_copy(
-            src_ref=src,
+            src_ref=lines,
             dst_ref=out.at[g],
-            send_sem=send.at[i],
-            recv_sem=recv.at[i],
+            send_sem=gs.at[i],
+            recv_sem=gr.at[i],
             device_id={"ga": lax.rem(g + i, n_ga)},
             device_id_type=pl.DeviceIdType.MESH,
         )
@@ -348,7 +371,7 @@
     ]
     for c in copies:
         c.start()
-    out[g] = src[...]
+    out[g] = lines[...]
     for c in copies:
         c.wait()
 
@@ -413,41 +436,29 @@
         name="block",
     )(k_at, k2_at, half, y_all, p_all, coulomb.reshape(1, g))
     line = (n, quarter, CAPQ * nt)
-    everything = pl.pallas_call(
-        functools.partial(third_kernel, n),
-        out_shape=shape((n * n, quarter, CAPQ * nt), F32),
-        in_specs=[VM],
+    lines = rows // 2 + per_dev // 2
+    each = line[1:]
+    full = pl.pallas_call(
+        functools.partial(tail_kernel, n, rows, per_dev),
+        out_shape=shape((n_ga, lines) + each, F32),
+        in_specs=[SM, SM, VM],
         out_specs=VM,
         scratch_shapes=[
             pltpu.VMEM(line, F32),
             pltpu.VMEM((2,) + line, F32),
             pltpu.VMEM(line, F32),
             pltpu.VMEM(line, F32),
+            pltpu.VMEM(line, jnp.int32),
+            pltpu.VMEM((n, 1 + per_dev // 2) + each, F32),
+            pltpu.VMEM((n, 1 + per_dev // 2) + each, F32),
+            pltpu.VMEM((lines,) + each, F32),
         ]
         + [pltpu.SemaphoreType.DMA((2,))] * 4
-        + gather_sems(n),
+        + [pltpu.SemaphoreType.DMA((n,))] * 2
+        + [pltpu.SemaphoreType.DMA((n_ga,))] * 2,
         compiler_params=params(2),
-        name="reduce_blocks",
-    )(block)
-    lines = rows // 2 + per_dev // 2
-    mine = pl.pallas_call(
-        functools.partial(select_kernel, n, rows, per_dev),
-        out_shape=shape((lines, quarter, 2 * nt), F32),
-        in_specs=[SM, SM, VM],
-        out_specs=VM,
-        scratch_shapes=[pltpu.VMEM((per_dev, quarter, nt), F32)],
-        compiler_params=pltpu.CompilerParams(vmem_limit_bytes=LIMIT),
-        name="select",
-    )(listed, at, everything)
-    full = pl.pallas_call(
-        functools.partial(fourth_kernel, n),
-        out_shape=shape((n_ga, lines, quarter, 2 * nt), F32),
-        in_specs=[VM],
-        out_specs=VM,
-        scratch_shapes=[pltpu.SemaphoreType.DMA((n_ga,))] * 2,
-        compiler_params=params(3),
-        name="gather_out",
-    )(mine)
+        name="tail",
+    )(k2_at, at, block)
     split = lambda v: jnp.concatenate([v[..., :nt], v[..., nt:]], axis=1)
     blocks = split(full[:, : rows // 2]).transpose(1, 0, 2, 3).reshape(rows, nt * nt)
     mirrored = split(full[:, rows // 2 :]).transpose(1, 3, 0, 2).reshape(per_dev, nt * nt)

time: 147 us -> 127 us (0.86)
  Pallas kernels: 134 us -> 114 us
    pallas_call x3 -> x1, Pallas kernels: 33.1 us -> 17.6 us  [per_device(): pl.pallas_call(functools.partial(tail_kernel, n, rows, per_dev), out_shap...]
    pallas_call x1, Pallas kernels: 48.1 us -> 44.4 us  [per_device(): pl.pallas_call(functools.partial(second_kernel, n, pieces), out_shape=[sh...]
where the time goes in v2:
time: 127 us; the launch traced here: 126 us
  Pallas kernels  114 us (90%)
  local copies, waits for them, and re-layouts  11.3 us (9%)
    pallas_call x1, Pallas kernels, per_device(): pl.pallas_call(functools.partial(second_kernel, n, pieces), out_shape=[sh...  44.4 us
    pallas_call x1, Pallas kernels, per_device(): pl.pallas_call(functools.partial(first_kernel, n), out_shape=[shape((n *...  30.7 us
    pallas_call x1, Pallas kernels, per_device(): pl.pallas_call(functools.partial(tail_kernel, n, rows, per_dev), out_shap...  17.6 us
    pallas_call x1, Pallas kernels, per_device(): pl.pallas_call(functools.partial(half_kernel, n, rows, q_slots), out_shap...  15.6 us
    pallas_call x1, Pallas kernels, per_device(): pl.pallas_call(functools.partial(block_kernel, n), out_shape=shape((n_ga,...  5.42 us
    unnamed x4, local copies, waits for them, and re-layouts  4.06 us

profile of v2, /device:TPU:0, one launch (start us, length us, event | category | flops | bytes accessed | tf_op | source)
XLA Modules:
  0.0 125.7 jit_solution(3597569200979213453)
XLA Ops:
  0.6 0.8 copy.15
  1.4 0.6 pad_bitcast_fusion.l_ref
  2.0 30.7 %gather_x.1 = (bf16[32,64,375]{2,1,0:T(8,128)(2,1)}, s32[16,8,128]{2,1,0:T(8,128)}) custom-call(bf16[4,64,375]{2,1,0:T(8,128)(2,1)} %x_ref.1, s32[2,8,128]{2,1,0:T(8,128)} %pad_bitcast_fusion.l_ref), custom_call_target="tpu_custom_call" | custom-call | tf_op jit(solution)/shard_map/gather_x/pallas_call | solution.py:388
  32.7 1.6 %reshape.24.list_ref = s32[384]{0:T(512)} reshape(s32[128,3]{1,0:T(8,128)} %bitcast.10) | data formatting | bytes 3072 | tf_op jit(solution)/shard_map/reshape | solution.py:397
  34.3 3.3 %copy.12.w_ref = bf16[2,375,1500]{2,1,0:T(8,128)(2,1)} copy(bf16[2,375,1500]{2,0,1:T(2,128)(2,1)} %param.11) | data formatting | bytes 4500000 | tf_op args[4]
  37.6 15.6 %half.1 = (f32[4,16,64,375]{3,2,1,0:T(8,128)}, s32[16]{0:T(128)}, s32[16]{0:T(128)}, s32[128]{0:T(128)}) custom-call(s32[384]{0:T(512)} %reshape.24.list_ref, s32[16]{0:T(128)} %qs_ref.1, bf16[32,64,375]{2,1,0:T(8,128)(2,1)} %get-tuple-element.12.x_ref, bf16[2,375,1500]{2,1,0:T(8,128)(2,1)} %copy.12.w_ref), custom_call_target="tpu_custom_call" | custom-call | tf_op jit(solution)/shard_map/half/pallas_call | solution.py:400
  53.2 0.0 copy-start
  53.2 44.4 %reduce_gather.1 = (bf16[16,64,375]{2,1,0:T(8,128)(2,1)}, bf16[32,64,375]{2,1,0:T(8,128)(2,1)}, bf16[32,64,375]{2,1,0:T(8,128)(2,1)}) custom-call(f32[4,16,64,375]{3,2,1,0:T(8,128)} %get-tuple-element.16.part, bf16[4,64,375]{2,1,0:T(8,128)(2,1)} %y_ref.1, bf16[4,64,375]{2,1,0:T(8,128)(2,1)} %p_ref.1), custom_call_target="tpu_custom_call" | custom-call | tf_op jit(solution)/shard_map/reduce_gather/pallas_call | solution.py:410
  97.6 0.0 copy-done
  97.6 0.6 reshape.25.v_ref
  98.2 5.4 %block.1.part = f32[4,8,16,128]{3,2,1,0:T(8,128)} custom-call(s32[16]{0:T(128)} %get-tuple-element.15.k_ref, s32[16]{0:T(128)} %get-tuple-element.13.k2_ref, bf16[16,64,375]{2,1,0:T(8,128)(2,1)} %get-tuple-element.17.half_ref, bf16[32,64,375]{2,1,0:T(8,128)(2,1)} %get-tuple-element.18.y_ref, bf16[32,64,375]{2,1,0:T(8,128)(2,1)} %get-tuple-element.19.p_ref, ...), custom_call_target="tpu_custom_call" | custom-call | tf_op jit(solution)/shard_map/block/pallas_call | solution.py:430
  103.6 17.6 %tail.1 = f32[4,10,16,128]{3,2,1,0:T(8,128)} custom-call(s32[16]{0:T(128)} %get-tuple-element.13.k2_ref, s32[128]{0:T(128)} %get-tuple-element.14.at_ref, f32[4,8,16,128]{3,2,1,0:T(8,128)} %block.1.part), custom_call_target="tpu_custom_call" | custom-call | tf_op jit(solution)/shard_map/tail/pallas_call | solution.py:441
  121.2 1.2 fusion.1
  122.5 0.9 reshape.26
  123.4 1.0 fusion
  124.4 0.2 copy.14
  124.6 1.1 reshape.27
  (3 shorter events, 0.1 us)
Async XLA Ops:
  53.2 44.4 %copy-start = (f32[375]{0:T(512)S(1)}, f32[375]{0:T(512)}, u32[]{:S(2)}) copy-start(f32[375]{0:T(512)} %param.10) | copy-start | bytes 4504

commit v3 on v2

--- a/solution.py
+++ b/solution.py
@@ -103,13 +103,11 @@
         lax.fori_loop(1, self.nz, tail, 0)
 
 
-def run_gathers(gathers, between=None):
+def run_gathers(gathers):
     for g in gathers:
         g.first()
     for g in gathers:
         g.second()
-    if between is not None:
-        between()
 
     def body(h, carry):
         for g in gathers:
@@ -156,7 +154,7 @@
     run_gathers([Gather(n, l_ref, lo_ref, ls, lr), Gather(n, x_ref, xo_ref, xs, xr)])
 
 
-def half_kernel(n, rows, q_slots, list_ref, qs_ref, x_ref, w_ref, o_ref, k_ref, k2_ref, at_ref, w_at, count):
+def table_kernel(n, rows, q_slots, list_ref, qs_ref, k_ref, k2_ref, at_ref, w_at, count):
     me = lax.axis_index("ka")
     slots = n * CAPQ
 
@@ -195,15 +193,6 @@
         return lax.fori_loop(0, rows, pair, c)
 
     lax.fori_loop(0, n, source, 0)
-    n_ga, g = o_ref.shape[0], o_ref.shape[3]
-
-    def multiply(s, c):
-        v = jnp.dot(x_ref[k_ref[s]], w_ref[w_at[s]], preferred_element_type=F32)
-        for i in range(n_ga):
-            o_ref[i, s] = v[:, i * g : (i + 1) * g].astype(o_ref.dtype)
-        return c
-
-    lax.fori_loop(0, slots, multiply, 0)
 
 
 def reduce_two(part, out, recv1, tsend, recv2, s1, r1, s2, r2, pieces):
@@ -234,11 +223,9 @@
             device_id_type=pl.DeviceIdType.MESH,
         )
 
-    def begin():
-        for i in range(pieces):
-            one(0, there, i).start()
-        for i in range(pieces):
-            one(1, here, i).start()
+    def begin(i):
+        one(0, there, i).start()
+        one(1, here, i).start()
 
     def middle():
         for i in range(pieces):
@@ -263,12 +250,38 @@
     return begin, middle, end
 
 
-def second_kernel(n, pieces, part, y_ref, p_ref, half_ref, yo_ref, po_ref, recv1, tsend, recv2,
-                  s1, r1, s2, r2, ys, yr, ps, pr):
+def second_kernel(n, pieces, k_ref, w_at, x_ref, w_ref, y_ref, p_ref, half_ref, yo_ref, po_ref, part,
+                  recv1, tsend, recv2, s1, r1, s2, r2, ys, yr, ps, pr):
     greet(n, True, True)
+    gathers = [Gather(n, y_ref, yo_ref, ys, yr), Gather(n, p_ref, po_ref, ps, pr)]
+    for g in gathers:
+        g.first()
     begin, middle, end = reduce_two(part, half_ref, recv1, tsend, recv2, s1, r1, s2, r2, pieces)
-    begin()
-    run_gathers([Gather(n, y_ref, yo_ref, ys, yr), Gather(n, p_ref, po_ref, ps, pr)], middle)
+    n_ga, width = part.shape[0], part.shape[3]
+    per = part.shape[1] // pieces
+
+    def multiply(s, c):
+        v = jnp.dot(x_ref[k_ref[s]], w_ref[w_at[s]], preferred_element_type=F32)
+        for i in range(n_ga):
+            part[i, s] = v[:, i * width : (i + 1) * width].astype(part.dtype)
+        return c
+
+    for i in range(pieces):
+        if i == pieces // 2:
+            for g in gathers:
+                g.second()
+        lax.fori_loop(i * per, (i + 1) * per, multiply, 0)
+        begin(i)
+    middle()
+
+    def body(h, carry):
+        for g in gathers:
+            g.hop(h)
+        return carry
+
+    lax.fori_loop(1, gathers[0].nz, body, 0)
+    for g in gathers:
+        g.finish()
     end()
 
 
@@ -301,7 +314,7 @@
                 outbox, inbox, lines, s1, r1, s2, r2, as_, ar, gs, gr):
     greet(n, False, True, True)
     begin, middle, end = reduce_two(part, own, recv1, tsend, recv2, s1, r1, s2, r2, 1)
-    begin()
+    begin(0)
     me = lax.axis_index("ka")
     g = lax.axis_index("ga")
     n_ga = out.shape[0]
@@ -397,22 +410,22 @@
     listed = listed.reshape(n * rows, 128)[:, :3].reshape(n * rows * 3)
     wide = F32 if slots * nt <= 2048 else BF16
     ints = lambda m: shape((m,), jnp.int32)
-    part, k_at, k2_at, at = pl.pallas_call(
-        functools.partial(half_kernel, n, rows, q_slots),
-        out_shape=[shape((n_ga, slots, nt, g), wide), ints(slots), ints(slots), ints(n * rows)],
-        in_specs=[SM, SM, VM, VM],
-        out_specs=[VM, SM, SM, SM],
-        scratch_shapes=[pltpu.SMEM((slots,), jnp.int32), pltpu.SMEM((n,), jnp.int32)],
-        compiler_params=pltpu.CompilerParams(vmem_limit_bytes=LIMIT),
-        name="half",
-    )(listed, q_slot, x_all, screened)
+    k_at, k2_at, at, w_at = pl.pallas_call(
+        functools.partial(table_kernel, n, rows, q_slots),
+        out_shape=[ints(slots), ints(slots), ints(n * rows), ints(slots)],
+        in_specs=[SM, SM],
+        out_specs=[SM] * 4,
+        scratch_shapes=[pltpu.SMEM((n,), jnp.int32)],
+        name="tables",
+    )(listed, q_slot)
     pieces = 4
     half, y_all, p_all = pl.pallas_call(
         functools.partial(second_kernel, n, pieces),
         out_shape=[shape((slots, nt, g), BF16)] + [shape((n * per_dev, nt, g), BF16)] * 2,
-        in_specs=[VM, VM, VM],
+        in_specs=[SM, SM, VM, VM, VM, VM],
         out_specs=[VM, VM, VM],
         scratch_shapes=[
+            pltpu.VMEM((n_ga, slots, nt, g), wide),
             pltpu.VMEM((2, slots, nt, g), wide),
             pltpu.VMEM((slots, nt, g), BF16),
             pltpu.VMEM((slots, nt, g), BF16),
@@ -425,7 +438,7 @@
         + gather_sems(n),
         compiler_params=params(1),
         name="reduce_gather",
-    )(part, y_dens, p_dens)
+    )(k_at, w_at, x_all, screened, y_dens, p_dens)
     quarter = nt // n_ga
     block = pl.pallas_call(
         functools.partial(block_kernel, n),

time: 127 us -> 116 us (0.913)
  Pallas kernels: 114 us -> 102 us
    pallas_call x1, Pallas kernels: 15.6 us -> 5 us  [per_device(): pl.pallas_call(functools.partial(table_kernel, n, rows, q_slots), out_sha...]
where the time goes in v3:
time: 116 us; the launch traced here: 114 us
  Pallas kernels  102 us (88%)
  local copies, waits for them, and re-layouts  11.2 us (10%)
    pallas_call x1, Pallas kernels, per_device(): pl.pallas_call(functools.partial(second_kernel, n, pieces), out_shape=[sh...  43.7 us
    pallas_call x1, Pallas kernels, per_device(): pl.pallas_call(functools.partial(first_kernel, n), out_shape=[shape((n *...  30.6 us
    pallas_call x1, Pallas kernels, per_device(): pl.pallas_call(functools.partial(tail_kernel, n, rows, per_dev), out_shap...  17.6 us
    pallas_call x1, Pallas kernels, per_device(): pl.pallas_call(functools.partial(block_kernel, n), out_shape=shape((n_ga,...  5.42 us
    pallas_call x1, Pallas kernels, per_device(): pl.pallas_call(functools.partial(table_kernel, n, rows, q_slots), out_sha...  5 us
    unnamed x4, local copies, waits for them, and re-layouts  4.04 us

profile of v3, /device:TPU:0, one launch (start us, length us, event | category | flops | bytes accessed | tf_op | source)
XLA Modules:
  0.0 114.3 jit_solution(13497227622506883544)
XLA Ops:
  0.6 0.8 copy.15
  1.4 0.6 pad_bitcast_fusion.l_ref
  2.0 30.6 %gather_x.1 = (bf16[32,64,375]{2,1,0:T(8,128)(2,1)}, s32[16,8,128]{2,1,0:T(8,128)}) custom-call(bf16[4,64,375]{2,1,0:T(8,128)(2,1)} %x_ref.1, s32[2,8,128]{2,1,0:T(8,128)} %pad_bitcast_fusion.l_ref), custom_call_target="tpu_custom_call" | custom-call | tf_op jit(solution)/shard_map/gather_x/pallas_call | solution.py:401
  32.6 1.6 %reshape.24.list_ref = s32[384]{0:T(512)} reshape(s32[128,3]{1,0:T(8,128)} %bitcast.10) | data formatting | bytes 3072 | tf_op jit(solution)/shard_map/reshape | solution.py:410
  34.2 5.0 %tables.1 = (s32[16]{0:T(128)}, s32[16]{0:T(128)}, s32[128]{0:T(128)}, s32[16]{0:T(128)}) custom-call(s32[384]{0:T(512)} %reshape.24.list_ref, s32[16]{0:T(128)} %qs_ref.1), custom_call_target="tpu_custom_call" | custom-call | tf_op jit(solution)/shard_map/tables/pallas_call | solution.py:413
  39.2 3.3 %copy.12.w_ref = bf16[2,375,1500]{2,1,0:T(8,128)(2,1)} copy(bf16[2,375,1500]{2,0,1:T(2,128)(2,1)} %param.11) | data formatting | bytes 4500000 | tf_op args[4]
  42.5 0.0 copy-start
  42.5 43.7 %reduce_gather.1 = (bf16[16,64,375]{2,1,0:T(8,128)(2,1)}, bf16[32,64,375]{2,1,0:T(8,128)(2,1)}, bf16[32,64,375]{2,1,0:T(8,128)(2,1)}) custom-call(s32[16]{0:T(128)} %get-tuple-element.14.k_ref, s32[16]{0:T(128)} %get-tuple-element.15.w_at, bf16[32,64,375]{2,1,0:T(8,128)(2,1)} %get-tuple-element.16.x_ref, bf16[2,375,1500]{2,1,0:T(8,128)(2,1)} %copy.12.w_ref, ...), custom_call_target="tpu_custom_call" | custom-call | tf_op jit(solution)/shard_map/reduce_gather/pallas_call | solution.py:422
  86.2 0.0 copy-done
  86.2 0.6 reshape.25.v_ref
  86.8 5.4 %block.1.part = f32[4,8,16,128]{3,2,1,0:T(8,128)} custom-call(s32[16]{0:T(128)} %get-tuple-element.14.k_ref, s32[16]{0:T(128)} %get-tuple-element.12.k2_ref, bf16[16,64,375]{2,1,0:T(8,128)(2,1)} %get-tuple-element.17.half_ref, bf16[32,64,375]{2,1,0:T(8,128)(2,1)} %get-tuple-element.18.y_ref, bf16[32,64,375]{2,1,0:T(8,128)(2,1)} %get-tuple-element.19.p_ref, ...), custom_call_target="tpu_custom_call" | custom-call | tf_op jit(solution)/shard_map/block/pallas_call | solution.py:443
  92.2 17.6 %tail.1 = f32[4,10,16,128]{3,2,1,0:T(8,128)} custom-call(s32[16]{0:T(128)} %get-tuple-element.12.k2_ref, s32[128]{0:T(128)} %get-tuple-element.13.at_ref, f32[4,8,16,128]{3,2,1,0:T(8,128)} %block.1.part), custom_call_target="tpu_custom_call" | custom-call | tf_op jit(solution)/shard_map/tail/pallas_call | solution.py:454
  109.9 1.2 %fusion.1 = (f32[4,8,16,64]{3,2,1,0:T(8,128)S(1)}, f32[4,8,16,64]{3,2,1,0:T(8,128)S(1)}) fusion(f32[4,10,16,128]{3,2,1,0:T(8,128)} %tail.1), kind=kLoop, calls=%fused_computation.4 | loop fusion | bytes 524288 | tf_op jit(solution)/shard_map/slice | solution.py:475
  111.1 0.9 reshape.26
  112.0 1.0 fusion
  113.0 0.2 copy.14
  113.3 1.1 reshape.27
  (3 shorter events, 0.1 us)
Async XLA Ops:
  42.5 43.7 %copy-start = (f32[375]{0:T(512)S(1)}, f32[375]{0:T(512)}, u32[]{:S(2)}) copy-start(f32[375]{0:T(512)} %param.10) | copy-start | bytes 4504
